TPU v7x, 128 devices: a whole 4x4x4 slice. The times are simulated.
128 devices in a mesh: seq: 16 (over z_hi, x, core), chan: 8 (over z_lo, y).
Axes of the slice: x: 4, y: 4, z: 4 (z_hi: 2, z_lo: 2; z = z_hi * 2 + z_lo), core: 2. Of those that a mesh axis runs over, the one named last changes fastest.
Arguments:
- hidden_states: bfloat16 [4096, 4096], P('chan', 'seq'), may hold values from -700 to 700
- norm_gain: float32 [4096], P('chan'), may hold values from 0.1 to 1.9
- short_filter: float32 [4096, 128], P('chan'), may hold values from -0.5 to 0.5
- long_filter: bfloat16 [4096, 4096], P('chan', 'seq'), may hold values from -0.09375 to 0.09375
- long_bias: float32 [4096], P('chan'), may hold values from -4 to 4
- gate_stream: bfloat16 [4096, 4096], P('chan', 'seq'), may hold values from -6 to 6
- upstream: bfloat16 [4096, 4096], P(None, 'seq'), may hold values from -6 to 6
Outputs:
- mixed: bfloat16 [4096, 4096], P('chan', 'seq')
- weight_grad: float32 [4096, 4096], P('seq', 'chan')
All inputs are finite; a program needn't handle non-finite values.
Results may differ from a plain program's by a relative error of at most 0.015.
Values may be sent and summed in bfloat16 or wider, within the bound.
No kernel may reach another device: no remote copies, remote signals or barrier semaphores. Data moves between devices by JAX's collectives and lax.ppermute only.
A program may use at most 64 MiB of HBM per device.

v0:
```python
import math
import jax
import jax.numpy as jnp
from jax import lax
from jax.sharding import PartitionSpec as P

D = 4096
EPSILON = 1e-05


def copy_for_each(value, axis):
    copies = jnp.broadcast_to(value, (lax.axis_size(axis), *value.shape))
    return lax.all_to_all(copies, axis, split_axis=0, concat_axis=0, tiled=True)


def over_copies(value, axis):
    everything = copy_for_each(value, axis)
    return jnp.sum(everything, axis=0)


def passed_along(value, axis, by):
    devices = lax.axis_size(axis)
    pairs = [(i, i + by) for i in range(devices) if 0 <= i + by < devices]
    return lax.ppermute(value, axis, pairs)


def short_conv(padded, taps):
    kernel = taps[:, ::-1][:, None, :]
    result = lax.conv_general_dilated(
        padded[None],
        kernel,
        (1,),
        "VALID",
        dimension_numbers=("NCH", "OIH", "NCH"),
        feature_group_count=padded.shape[0],
        precision=lax.Precision.HIGHEST,
    )
    return result[0]


def twiddle(row_total, col_total, modulus, direction):
    product = (
        jnp.arange(row_total, dtype=jnp.int32)[:, None]
        * jnp.arange(col_total, dtype=jnp.int32)[None, :]
        % modulus
    )
    angles = direction * 2.0 * math.pi * product.astype(jnp.float32) / modulus
    return (jnp.cos(angles), jnp.sin(angles))


def product_einsum(form, left, right):
    return jnp.einsum(form, left, right, precision=lax.Precision.HIGHEST)


def split_table(table):
    upper = table.astype(jnp.bfloat16)
    lower = (table - upper.astype(jnp.float32)).astype(jnp.bfloat16)
    return (upper, lower)


def table_product(table, grid):
    upper, lower = split_table(table)
    first = jnp.einsum("kn,cnm->ckm", upper, grid, preferred_element_type=jnp.float32)
    return first + jnp.einsum("kn,cnm->ckm", lower, grid, preferred_element_type=jnp.float32)


def forward_real(signal, factor_a, factor_b):
    length = factor_a * factor_b
    seq_total = signal.shape[1]
    kept_in = -(-seq_total // factor_b)
    filled = jnp.pad(signal, ((0, 0), (0, kept_in * factor_b - seq_total)))
    grid = filled.reshape(signal.shape[0], kept_in, factor_b)
    outer_re, outer_im = twiddle(factor_a, kept_in, factor_a, -1.0)
    section_re = table_product(outer_re, grid)
    section_im = table_product(outer_im, grid)
    turn_re, turn_im = twiddle(factor_a, factor_b, length, -1.0)
    rotated_re = section_re * turn_re - section_im * turn_im
    rotated_im = section_re * turn_im + section_im * turn_re
    inner_re, inner_im = twiddle(factor_b, factor_b, factor_b, -1.0)
    result_re = product_einsum("ckm,jm->ckj", rotated_re, inner_re) - product_einsum(
        "ckm,jm->ckj", rotated_im, inner_im
    )
    result_im = product_einsum("ckm,jm->ckj", rotated_re, inner_im) + product_einsum(
        "ckm,jm->ckj", rotated_im, inner_re
    )
    return (result_re, result_im)


def inverse_real(spec_re, spec_im, factor_a, factor_b, kept_rows):
    length = factor_a * factor_b
    inner_re, inner_im = twiddle(factor_b, factor_b, factor_b, 1.0)
    section_re = product_einsum("ckj,mj->ckm", spec_re, inner_re) - product_einsum(
        "ckj,mj->ckm", spec_im, inner_im
    )
    section_im = product_einsum("ckj,mj->ckm", spec_re, inner_im) + product_einsum(
        "ckj,mj->ckm", spec_im, inner_re
    )
    turn_re, turn_im = twiddle(factor_a, factor_b, length, 1.0)
    rotated_re = section_re * turn_re - section_im * turn_im
    rotated_im = section_re * turn_im + section_im * turn_re
    outer_re, outer_im = twiddle(kept_rows, factor_a, factor_a, 1.0)
    result = product_einsum("nk,ckm->cnm", outer_re, rotated_re) - product_einsum(
        "nk,ckm->cnm", outer_im, rotated_im
    )
    return result.reshape(result.shape[0], kept_rows * factor_b) / length


def long_convolution(signal, filt):
    seq_total = signal.shape[1]
    length = 2 * seq_total
    factor_a = 1
    for divisor in range(1, math.isqrt(length) + 1):
        if length % divisor == 0:
            factor_a = divisor
    factor_b = length // factor_a
    signal_re, signal_im = forward_real(signal, factor_a, factor_b)
    filter_re, filter_im = forward_real(filt, factor_a, factor_b)
    joint_re = signal_re * filter_re - signal_im * filter_im
    joint_im = signal_re * filter_im + signal_im * filter_re
    kept_rows = -(-seq_total // factor_b)
    return inverse_real(joint_re, joint_im, factor_a, factor_b, kept_rows)[:, :seq_total]


def shards(hidden_states, norm_gain, short_filter, long_filter, long_bias, gate_stream, upstream):
    states = hidden_states.astype(jnp.float32)
    partial_squares = jnp.sum(states * states, axis=0)
    squares = over_copies(partial_squares, "chan")
    normed = (states * lax.rsqrt(squares / D + EPSILON)[None, :] * norm_gain[:, None]).astype(
        jnp.bfloat16
    )
    tap_count = short_filter.shape[1]
    width_local = hidden_states.shape[0] // lax.axis_size("seq")
    owner_index = lax.axis_index("seq")
    bias_slice = lax.dynamic_slice_in_dim(long_bias, owner_index * width_local, width_local)
    tail_cols = normed[:, normed.shape[1] - tap_count :]
    from_left = passed_along(tail_cols, "seq", 1)
    padded = jnp.concatenate(
        [from_left[:, 1:].astype(jnp.float32), normed.astype(jnp.float32)], axis=1
    )
    short_out = short_conv(padded, short_filter).astype(jnp.bfloat16)
    short_whole, filter_whole = (
        lax.all_to_all(short_out, "seq", split_axis=0, concat_axis=1, tiled=True),
        lax.all_to_all(long_filter, "seq", split_axis=0, concat_axis=1, tiled=True),
    )
    long_conv = long_convolution(short_whole, filter_whole)
    long_whole = (long_conv + bias_slice[:, None] * short_whole.astype(jnp.float32)).astype(
        jnp.bfloat16
    )
    long_out = lax.all_to_all(long_whole, "seq", split_axis=1, concat_axis=0, tiled=True)
    mixed = (gate_stream.astype(jnp.float32) * long_out.astype(jnp.float32)).astype(jnp.bfloat16)
    mixed_whole = lax.all_gather(mixed, "seq", axis=1, tiled=True)
    owned = lax.all_to_all(upstream, "seq", split_axis=0, concat_axis=1, tiled=True)
    weight_grad = lax.dot_general(
        owned, mixed_whole, (((1,), (1,)), ((), ())), preferred_element_type=jnp.float32
    )
    return (mixed, weight_grad)


def solution(mesh):
    placed = (
        P("chan", "seq"),
        P("chan"),
        P("chan", None),
        P("chan", "seq"),
        P("chan"),
        P("chan", "seq"),
        P(None, "seq"),
    )
    return jax.shard_map(
        shards,
        mesh=mesh,
        in_specs=placed,
        out_specs=(P("chan", "seq"), P("seq", "chan")),
        check_vma=False,
    )
```

profile of v0, /device:TPU:1, one launch (start us, length us, event | category | flops | bytes accessed | tf_op | source)
XLA Modules:
  0.0 171.9 jit_solution(16711213002969897261)
XLA Ops:
  8.2 11.2 %all_to_all.64 = f32[8,1,256]{2,1,0:T(1,128)S(1)} all-to-all(f32[8,1,256]{2,1,0:T(1,128)S(1)} %broadcast_in_dim.9), channel_id=1, replica_groups=mesh['seq'=16,'chan'=8] {'chan'}, dimensions={0} | all-to-all | bytes 16384 | tf_op jit(solution)/shard_map/all_to_all | solution.py:13
  19.4 9.4 %all-to-all-start.2 = ((bf16[16,32,256]{2,1,0:T(8,128)(2,1)}), bf16[16,32,256]{2,1,0:T(8,128)(2,1)S(1)}, u32[]{:S(2)}, u32[]{:S(2)}) async-start(bf16[16,32,256]{2,1,0:T(8,128)(2,1)} %bitcast.111), calls=%async_computation.2 | async-start | bytes 524288 | tf_op jit(solution)/shard_map/all_to_all | solution.py:143
  30.0 3.5 %collective-permute-start = (bf16[512,128]{1,0:T(8,128)(2,1)S(1)}, bf16[512,128]{1,0:T(8,128)(2,1)S(1)}, u32[]{:S(2)}, u32[]{:S(2)}) collective-permute-start(bf16[512,128]{1,0:T(8,128)(2,1)S(1)} %slice.8), channel_id=1, source_target_pairs={{0,8},{8,16},{16,24},{24,32},{32,40},{40,48},{48,56},{56,64},{64,7... | collective-permute-start | bytes 393224 | tf_op jit(solution)/shard_map/ppermute | solution.py:24
  33.7 1.9 %rev.3 = f32[512,128]{1,0:T(8,128)S(1)} reverse(f32[512,128]{1,0:T(8,128)} %param.9), dimensions={1} | reverse | bytes 524288 | tf_op jit(solution)/shard_map/rev | solution.py:28
  38.2 8.4 %convolution_convert_fusion = bf16[1,512,256]{1,0,2:T(2,128)(2,1)S(1)} fusion(bf16[1,512,383]{1,0,2:T(2,128)(2,1)S(1)} %copy.48, f32[512,1,128]{0,1,2:T(1,128)S(1)} %copy.49), kind=kOutput, calls=%fused_computation.12 | convolution fusion | flops 201457664 | bytes 916480 | tf_op jit(solution)/shard_map/conv_general_dilated | solution.py:29
  47.7 8.0 %all-to-all-start.1 = ((bf16[16,32,256]{2,1,0:T(8,128)(2,1)}), bf16[16,32,256]{2,1,0:T(8,128)(2,1)S(1)}, u32[]{:S(2)}, u32[]{:S(2)}) async-start(bf16[16,32,256]{2,1,0:T(8,128)(2,1)} %bitcast.2), calls=%async_computation.1 | async-start | bytes 524288 | tf_op jit(solution)/shard_map/all_to_all | solution.py:142
  57.9 1.2 fusion.6
  59.1 1.2 fusion.8
  60.3 1.2 convolution_add_fusion.1
  61.6 1.2 convolution_subtract_fusion.1
  62.9 1.6 all-to-all-done.1
  66.4 1.2 fusion.27
  67.6 1.3 fusion.26
  68.9 1.3 convolution_subtract_fusion.2
  70.2 1.7 %multiply_add_fusion = (f32[32,64,128]{2,1,0:T(8,128)S(1)}, f32[32,64,128]{2,1,0:T(8,128)S(1)}) fusion(f32[32,64,128]{2,1,0:T(8,128)S(1)} %convolution_subtract_fusion.1, f32[32,64,128]{2,1,0:T(8,128)S(1)} %convolution_subtract_fusion.2, f32[32,64,128]{2,1,0:T(8,128)S(1)} %convolution_add_fusion.1, f32[32,64,128]{2,1,0:T(8,128)S(1)} %fusion.26, ...), kind=kOutput, calls=%fused_computation.30 | convolution fusion | flops 405504000 | bytes 8454144 | tf_op jit(solution)/shard_map/ckm,jm->ckj/dot_general | solution.py:52
  71.9 1.2 fusion.34
  73.2 1.2 fusion.30
  74.4 1.3 convolution_subtract_fusion
  75.7 1.2 convolution_add_fusion
  79.2 14.1 %all_to_all.65 = bf16[32,16,256]{2,0,1:T(8,128)(2,1)S(1)} all-to-all(bf16[32,16,256]{2,0,1:T(8,128)(2,1)S(1)} %fusion.21), channel_id=1, replica_groups=mesh['seq'=16,'chan'=8] {'seq'}, dimensions={1} | all-to-all | bytes 524288 | tf_op jit(solution)/shard_map/all_to_all | solution.py:149
  94.2 36.4 %all_to_all.66 = bf16[16,256,256]{2,1,0:T(8,128)(2,1)S(1)} all-to-all(bf16[16,256,256]{2,1,0:T(8,128)(2,1)} %bitcast.107), channel_id=1, replica_groups=mesh['seq'=16,'chan'=8] {'seq'}, dimensions={0} | all-to-all | bytes 4194304 | tf_op jit(solution)/shard_map/all_to_all | solution.py:152
  130.6 2.4 %copy.54 = bf16[256,16,256]{0,2,1:T(8,128)(2,1)} copy(bf16[256,16,256]{2,0,1:T(8,128)(2,1)S(1)} %bitcast.105) | data formatting | bytes 4194304 | tf_op jit(solution)/shard_map/all_to_all | solution.py:152
  132.9 27.0 %all-gather.2.cloned.1.call-done = bf16[512,4096]{1,0:T(8,128)(2,1)} async-done(((bf16[512,256]{1,0:T(8,128)(2,1)}), bf16[512,4096]{1,0:T(8,128)(2,1)}) %all-gather.2.cloned.1.call-update) | async-done | bytes 4194320 | tf_op jit(solution)/shard_map/all_gather | solution.py:151
  159.9 4.1 %convolution_bitcast_fusion = f32[256,512]{0,1:T(8,128)S(1)} fusion(bf16[512,4096]{1,0:T(8,128)(2,1)} %all-gather.2.cloned.1.call-done, bf16[256,4096]{0,1:T(8,128)(2,1)} %bitcast.108), kind=kOutput, calls=%fused_computation.13 | convolution fusion | flops 1073741824 | bytes 6815744 | tf_op jit(solution)/shard_map/dot_general | solution.py:153
  (38 shorter events, 14.0 us)
Async XLA Ops:
  19.4 28.3 %all-to-all-start.2 = ((bf16[16,32,256]{2,1,0:T(8,128)(2,1)}), bf16[16,32,256]{2,1,0:T(8,128)(2,1)S(1)}, u32[]{:S(2)}, u32[]{:S(2)}) async-start(bf16[16,32,256]{2,1,0:T(8,128)(2,1)} %bitcast.111), calls=%async_computation.2 | async-start | bytes 524288 | tf_op jit(solution)/shard_map/all_to_all | solution.py:143
  30.0 6.7 %collective-permute-start = (bf16[512,128]{1,0:T(8,128)(2,1)S(1)}, bf16[512,128]{1,0:T(8,128)(2,1)S(1)}, u32[]{:S(2)}, u32[]{:S(2)}) collective-permute-start(bf16[512,128]{1,0:T(8,128)(2,1)S(1)} %slice.8), channel_id=1, source_target_pairs={{0,8},{8,16},{16,24},{24,32},{32,40},{40,48},{48,56},{56,64},{64,7... | collective-permute-start | bytes 393224 | tf_op jit(solution)/shard_map/ppermute | solution.py:24
  47.7 16.7 %all-to-all-start.1 = ((bf16[16,32,256]{2,1,0:T(8,128)(2,1)}), bf16[16,32,256]{2,1,0:T(8,128)(2,1)S(1)}, u32[]{:S(2)}, u32[]{:S(2)}) async-start(bf16[16,32,256]{2,1,0:T(8,128)(2,1)} %bitcast.2), calls=%async_computation.1 | async-start | bytes 524288 | tf_op jit(solution)/shard_map/all_to_all | solution.py:142
  55.8 104.2 %all-gather.2.cloned.1.call-start = ((), (), s32[]{:S(2)}) async-start(), calls=%async_computation.5 | async-start | bytes 4456448 | tf_op jit(solution)/shard_map/all_gather | solution.py:151
  78.7 14.6 %copy-start = (bf16[512,256]{1,0:T(8,128)(2,1)S(1)}, bf16[512,256]{1,0:T(8,128)(2,1)}, u32[]{:S(2)}) copy-start(bf16[512,256]{1,0:T(8,128)(2,1)} %param.12) | copy-start | bytes 786436
Sparse Core Ops, SparseCore 0:
  94.3 65.6 all-gather.1
where the time goes:
time: 173 us; the launch traced here: 172 us
  blocking collectives  61.7 us (36%)
  matrix products  33.1 us (19%)
  waiting for transfers between devices  28.6 us (17%)
  starting transfers between devices  21.2 us (12%)
  between operations  14.3 us (8%)
  local copies, waits for them, and re-layouts  9.21 us (5%)
  other arithmetic  3.75 us (2%)
    all_to_all x1, blocking collectives, shards(): lax.all_to_all(upstream, 'seq', split_axis=0, concat_axis=1, tiled=True)  36.4 us
    all_gather x1, waiting for transfers between devices, shards(): mixed_whole = lax.all_gather(mixed, 'seq', axis=1, tiled=True)  27 us
    dot_general x14, matrix products, product_einsum(): return jnp.einsum(form, left, right, precision=lax.Precision.HIGHEST)  17.2 us
    all_to_all x1, blocking collectives, shards(): lax.all_to_all(long_whole, 'seq', split_axis=1, concat_axis=0, tiled=True)  14.1 us
    all_to_all x1, blocking collectives, copy_for_each(): return lax.all_to_all(copies, axis, split_axis=0, concat_axis=0, tiled=True)  11.2 us
    all_to_all x1, starting transfers between devices, shards(): lax.all_to_all(long_filter, 'seq', split_axis=0, concat_axis=1, tiled=True)  9.44 us
    conv_general_dilated x1, matrix products, short_conv(): lax.conv_general_dilated(padded[None], kernel, (1,), 'VALID', dimension_n...  8.45 us
    all_to_all x1, starting transfers between devices, shards(): lax.all_to_all(short_out, 'seq', split_axis=0, concat_axis=1, tiled=True)  8 us
  transfers between devices with their start and end apart: 4, of which 2 were waited for; matrix products, arithmetic and copies ran while one was open for 14% of the time, Pallas kernels for 0%

commit v1 on v0

--- a/solution.py
+++ b/solution.py
@@ -6,6 +6,13 @@
 
 D = 4096
 EPSILON = 1e-05
+
+
+def exchange_gather(array, name, dim):
+    devices = lax.axis_size(name)
+    blocks = jnp.stack([array for _ in range(devices)])
+    blocks = lax.all_to_all(blocks, name, split_axis=0, concat_axis=0)
+    return jnp.concatenate(blocks, axis=dim)
 
 
 def copy_for_each(value, axis):
@@ -148,7 +155,7 @@
     )
     long_out = lax.all_to_all(long_whole, "seq", split_axis=1, concat_axis=0, tiled=True)
     mixed = (gate_stream.astype(jnp.float32) * long_out.astype(jnp.float32)).astype(jnp.bfloat16)
-    mixed_whole = lax.all_gather(mixed, "seq", axis=1, tiled=True)
+    mixed_whole = exchange_gather(mixed, "seq", 1)
     owned = lax.all_to_all(upstream, "seq", split_axis=0, concat_axis=1, tiled=True)
     weight_grad = lax.dot_general(
         owned, mixed_whole, (((1,), (1,)), ((), ())), preferred_element_type=jnp.float32

time: 173 us -> 178 us (1.029)
  blocking collectives: 61.7 us -> 80.5 us
  between operations: 14.3 us -> 0.95 us
  starting transfers between devices: 21.2 us -> 25.2 us
  matrix products: 33.1 us -> 29.8 us
  local copies, waits for them, and re-layouts: 9.21 us -> 7.25 us
  waiting for transfers between devices: 28.6 us -> 30.4 us
    all_to_all x0 -> x1, waiting for transfers between devices: none -> 28.5 us  [shards(): lax.all_to_all(upstream, 'seq', split_axis=0, concat_axis=1, tiled=True)]
    all_gather x1 -> x0, waiting for transfers between devices: 27 us -> none  [shards(): mixed_whole = lax.all_gather(mixed, 'seq', axis=1, tiled=True)]
    all_to_all x1, blocking collectives: 36.4 us -> 55.4 us  [exchange_gather(): blocks = lax.all_to_all(blocks, name, split_axis=0, concat_axis=0)]
    all_to_all x0 -> x1, starting transfers between devices: none -> 4.25 us  [shards(): lax.all_to_all(upstream, 'seq', split_axis=0, concat_axis=1, tiled=True)]
    dot_general x1, matrix products: 4.11 us -> 1.28 us  [shards(): lax.dot_general(owned, mixed_whole, (((1,), (1,)), ((), ())), preferred_e...]
    all_to_all x1 -> x0, local copies, waits for them, and re-layouts: 2.37 us -> none  [shards(): lax.all_to_all(upstream, 'seq', split_axis=0, concat_axis=1, tiled=True)]
  transfers between devices with their start and end apart: 4 -> 4, of which waited for: 2 -> 2; matrix products, arithmetic and copies ran while one was open for 14% -> 12% of each run, Pallas kernels for 0% -> 0%
where the time goes in v1:
time: 178 us; the launch traced here: 177 us
  blocking collectives  80.5 us (45%)
  waiting for transfers between devices  30.4 us (17%)
  matrix products  29.8 us (17%)
  starting transfers between devices  25.2 us (14%)
  local copies, waits for them, and re-layouts  7.25 us (4%)
  other arithmetic  3.05 us (2%)
    all_to_all x1, blocking collectives, exchange_gather(): blocks = lax.all_to_all(blocks, name, split_axis=0, concat_axis=0)  55.4 us
    all_to_all x1, waiting for transfers between devices, shards(): lax.all_to_all(upstream, 'seq', split_axis=0, concat_axis=1, tiled=True)  28.5 us
    dot_general x14, matrix products, product_einsum(): return jnp.einsum(form, left, right, precision=lax.Precision.HIGHEST)  17.1 us
    all_to_all x1, blocking collectives, shards(): lax.all_to_all(long_whole, 'seq', split_axis=1, concat_axis=0, tiled=True)  13.9 us
    all_to_all x1, blocking collectives, copy_for_each(): return lax.all_to_all(copies, axis, split_axis=0, concat_axis=0, tiled=True)  11.2 us
    all_to_all x1, starting transfers between devices, shards(): lax.all_to_all(long_filter, 'seq', split_axis=0, concat_axis=1, tiled=True)  9.44 us
    conv_general_dilated x1, matrix products, short_conv(): lax.conv_general_dilated(padded[None], kernel, (1,), 'VALID', dimension_n...  8.08 us
    all_to_all x1, starting transfers between devices, shards(): lax.all_to_all(short_out, 'seq', split_axis=0, concat_axis=1, tiled=True)  8 us
  transfers between devices with their start and end apart: 4, of which 2 were waited for; matrix products, arithmetic and copies ran while one was open for 12% of the time, Pallas kernels for 0%

profile of v1, /device:TPU:1, one launch (start us, length us, event | category | flops | bytes accessed | tf_op | source)
XLA Modules:
  0.0 177.1 jit_solution(10999091406086390878)
XLA Ops:
  1.7 11.2 %all_to_all.66 = f32[8,1,256]{2,1,0:T(1,128)S(1)} all-to-all(f32[8,1,256]{2,1,0:T(1,128)S(1)} %broadcast_in_dim.9), channel_id=1, replica_groups=mesh['seq'=16,'chan'=8] {'chan'}, dimensions={0} | all-to-all | bytes 16384 | tf_op jit(solution)/shard_map/all_to_all | solution.py:20
  12.9 9.4 %all-to-all-start.2 = ((bf16[16,32,256]{2,1,0:T(8,128)(2,1)}), bf16[16,32,256]{2,1,0:T(8,128)(2,1)S(1)}, u32[]{:S(2)}, u32[]{:S(2)}) async-start(bf16[16,32,256]{2,1,0:T(8,128)(2,1)} %bitcast.116), calls=%async_computation.2 | async-start | bytes 524288 | tf_op jit(solution)/shard_map/all_to_all | solution.py:150
  23.5 3.5 %collective-permute-start = (bf16[512,128]{1,0:T(8,128)(2,1)S(1)}, bf16[512,128]{1,0:T(8,128)(2,1)S(1)}, u32[]{:S(2)}, u32[]{:S(2)}) collective-permute-start(bf16[512,128]{1,0:T(8,128)(2,1)S(1)} %slice.8), channel_id=1, source_target_pairs={{0,8},{8,16},{16,24},{24,32},{32,40},{40,48},{48,56},{56,64},{64,7... | collective-permute-start | bytes 393224 | tf_op jit(solution)/shard_map/ppermute | solution.py:31
  27.2 1.9 %rev.3 = f32[512,128]{1,0:T(8,128)S(1)} reverse(f32[512,128]{1,0:T(8,128)} %param.9), dimensions={1} | reverse | bytes 524288 | tf_op jit(solution)/shard_map/rev | solution.py:35
  31.6 8.1 %convolution_convert_fusion = bf16[1,512,256]{1,0,2:T(2,128)(2,1)S(1)} fusion(bf16[1,512,383]{1,0,2:T(2,128)(2,1)S(1)} %copy.38, f32[512,1,128]{0,1,2:T(1,128)S(1)} %copy.39), kind=kOutput, calls=%fused_computation.15 | convolution fusion | flops 201457664 | bytes 916480 | tf_op jit(solution)/shard_map/conv_general_dilated | solution.py:36
  40.8 8.0 %all-to-all-start.1 = ((bf16[16,32,256]{2,1,0:T(8,128)(2,1)}), bf16[16,32,256]{2,1,0:T(8,128)(2,1)S(1)}, u32[]{:S(2)}, u32[]{:S(2)}) async-start(bf16[16,32,256]{2,1,0:T(8,128)(2,1)} %bitcast.2), calls=%async_computation.1 | async-start | bytes 524288 | tf_op jit(solution)/shard_map/all_to_all | solution.py:149
  50.7 1.2 fusion.14
  52.0 1.2 fusion.16
  53.2 1.2 convolution_add_fusion.1
  54.5 1.2 convolution_subtract_fusion.1
  55.7 1.9 %all-to-all-done.1 = bf16[16,32,256]{2,1,0:T(8,128)(2,1)S(1)} async-done(((bf16[16,32,256]{2,1,0:T(8,128)(2,1)}), bf16[16,32,256]{2,1,0:T(8,128)(2,1)S(1)}, u32[]{:S(2)}, u32[]{:S(2)}) %all-to-all-start.1) | async-done | bytes 262176 | tf_op jit(solution)/shard_map/all_to_all | solution.py:149
  59.5 1.2 fusion.35
  60.7 1.3 fusion.34
  62.0 1.3 convolution_subtract_fusion.2
  63.3 1.7 multiply_add_fusion
  65.0 1.2 fusion.42
  66.2 1.2 fusion.38
  67.5 1.3 convolution_subtract_fusion
  68.7 1.2 convolution_add_fusion
  72.3 13.9 %all_to_all.67 = bf16[32,16,256]{2,0,1:T(8,128)(2,1)S(1)} all-to-all(bf16[32,16,256]{2,0,1:T(8,128)(2,1)S(1)} %fusion.29), channel_id=1, replica_groups=mesh['seq'=16,'chan'=8] {'seq'}, dimensions={1} | all-to-all | bytes 524288 | tf_op jit(solution)/shard_map/all_to_all | solution.py:156
  86.2 4.3 %all-to-all-start.5 = ((bf16[16,256,256]{2,1,0:T(8,128)(2,1)}), bf16[16,256,256]{2,1,0:T(8,128)(2,1)S(1)}, u32[]{:S(2)}, u32[]{:S(2)}) async-start(bf16[16,256,256]{2,1,0:T(8,128)(2,1)} %bitcast.24), calls=%async_computation.5 | async-start | bytes 4194304 | tf_op jit(solution)/shard_map/all_to_all | solution.py:159
  90.5 28.5 %all-to-all-done.5 = bf16[16,256,256]{2,1,0:T(8,128)(2,1)S(1)} async-done(((bf16[16,256,256]{2,1,0:T(8,128)(2,1)}), bf16[16,256,256]{2,1,0:T(8,128)(2,1)S(1)}, u32[]{:S(2)}, u32[]{:S(2)}) %all-to-all-start.5) | async-done | bytes 2097184 | tf_op jit(solution)/shard_map/all_to_all | solution.py:159
  119.4 55.4 %all_to_all.68 = bf16[16,512,256]{2,1,0:T(8,128)(2,1)S(1)} all-to-all(bf16[16,512,256]{2,1,0:T(8,128)(2,1)S(1)} %stack.2), channel_id=1, replica_groups=mesh['seq'=16,'chan'=8] {'seq'}, dimensions={0} | all-to-all | bytes 8388608 | tf_op jit(solution)/shard_map/all_to_all | solution.py:14
  174.9 1.3 fusion.5
  (39 shorter events, 13.4 us)
Async XLA Ops:
  12.9 28.0 %all-to-all-start.2 = ((bf16[16,32,256]{2,1,0:T(8,128)(2,1)}), bf16[16,32,256]{2,1,0:T(8,128)(2,1)S(1)}, u32[]{:S(2)}, u32[]{:S(2)}) async-start(bf16[16,32,256]{2,1,0:T(8,128)(2,1)} %bitcast.116), calls=%async_computation.2 | async-start | bytes 524288 | tf_op jit(solution)/shard_map/all_to_all | solution.py:150
  23.5 6.7 %collective-permute-start = (bf16[512,128]{1,0:T(8,128)(2,1)S(1)}, bf16[512,128]{1,0:T(8,128)(2,1)S(1)}, u32[]{:S(2)}, u32[]{:S(2)}) collective-permute-start(bf16[512,128]{1,0:T(8,128)(2,1)S(1)} %slice.8), channel_id=1, source_target_pairs={{0,8},{8,16},{16,24},{24,32},{32,40},{40,48},{48,56},{56,64},{64,7... | collective-permute-start | bytes 393224 | tf_op jit(solution)/shard_map/ppermute | solution.py:31
  40.8 16.7 %all-to-all-start.1 = ((bf16[16,32,256]{2,1,0:T(8,128)(2,1)}), bf16[16,32,256]{2,1,0:T(8,128)(2,1)S(1)}, u32[]{:S(2)}, u32[]{:S(2)}) async-start(bf16[16,32,256]{2,1,0:T(8,128)(2,1)} %bitcast.2), calls=%async_computation.1 | async-start | bytes 524288 | tf_op jit(solution)/shard_map/all_to_all | solution.py:149
  71.8 18.6 %copy-start.1 = (bf16[512,256]{1,0:T(8,128)(2,1)S(1)}, bf16[512,256]{1,0:T(8,128)(2,1)}, u32[]{:S(2)}) copy-start(bf16[512,256]{1,0:T(8,128)(2,1)} %param.12) | copy-start | bytes 786436
  86.2 32.9 %all-to-all-start.5 = ((bf16[16,256,256]{2,1,0:T(8,128)(2,1)}), bf16[16,256,256]{2,1,0:T(8,128)(2,1)S(1)}, u32[]{:S(2)}, u32[]{:S(2)}) async-start(bf16[16,256,256]{2,1,0:T(8,128)(2,1)} %bitcast.24), calls=%async_computation.5 | async-start | bytes 4194304 | tf_op jit(solution)/shard_map/all_to_all | solution.py:159
  90.5 84.4 %copy-start = (bf16[512,256]{1,0:T(8,128)(2,1)}, bf16[512,256]{1,0:T(8,128)(2,1)S(1)}, u32[]{:S(2)}) copy-start(bf16[512,256]{1,0:T(8,128)(2,1)S(1)} %fusion.28) | copy-start | bytes 786436
